TPU v7x, 32 devices: a whole 2x2x4 slice. The times are simulated.
32 devices in a mesh: cuts: 4 (over z), dp: 4 (over y, x), mp: 2 (over core).
Axes of the slice: x: 2, y: 2, z: 4, core: 2. Of those that a mesh axis runs over, the one named last changes fastest.
Arguments:
- attn_out: bfloat16 [2048, 3072], P(('cuts', 'dp'), 'mp'), may hold values from -6 to 6
- out_weight: bfloat16 [3072, 6144], P('mp'), may hold values from -0.109375 to 0.109375
- residual: bfloat16 [2048, 6144], P(('cuts', 'dp', 'mp')), may hold values from -45 to 45
- target: bfloat16 [2048, 6144], P(('cuts', 'dp', 'mp')), may hold values from -5 to 5
- norm_gain: float32 [6144], replicated, may hold values from 0.1 to 1.9
Outputs:
- block_out: bfloat16 [2048, 6144], P(('cuts', 'dp', 'mp'))
- attn_grad: bfloat16 [2048, 3072], P(('cuts', 'dp'), 'mp')
- weight_grad: float32 [3072, 6144], P('mp', 'dp')
All inputs are finite; a program needn't handle non-finite values.
Results may differ from a plain program's by a relative error of at most 0.018.
Values may be sent and summed in bfloat16 or wider, within the bound.
A program may use at most 128 MiB of HBM per device.

v0:
```python
import jax
import jax.numpy as jnp
from jax import lax
from jax.sharding import PartitionSpec as P

epsilon = 1e-06


def norm_backward(stream, target, norm_gain):
    center = stream - jnp.mean(stream, axis=1, keepdims=True)
    inv_std = lax.rsqrt(jnp.mean(center * center, axis=1, keepdims=True) + epsilon)
    normed = center * inv_std
    misfit = normed * norm_gain[None, :] - target.astype(jnp.float32)
    gain_err = misfit * norm_gain[None, :]
    bracket = (
        gain_err
        - jnp.mean(gain_err, axis=1, keepdims=True)
        - normed * jnp.mean(gain_err * normed, axis=1, keepdims=True)
    )
    return (inv_std * bracket).astype(jnp.bfloat16)


def per_device(attn_out, out_weight, residual, target, norm_gain):
    tokens_dev = attn_out.shape[0]
    head_cols = attn_out.shape[1]
    replica_scale = 1.0 / (lax.axis_size("cuts") * lax.axis_size("dp"))
    summed = lax.psum_scatter(
        jnp.dot(attn_out, out_weight, preferred_element_type=jnp.float32).astype(jnp.bfloat16),
        "mp",
        scatter_dimension=0,
        tiled=True,
    ).astype(jnp.float32)
    stream = summed + residual.astype(jnp.float32)
    block_out = stream.astype(jnp.bfloat16)
    cotangent = norm_backward(stream, target, norm_gain)
    portion = lax.all_gather(cotangent, "mp", axis=0, tiled=True)
    stored = portion
    act_acc = lax.dot_general(
        portion, out_weight, (((1,), (1,)), ((), ())), preferred_element_type=jnp.float32
    )
    collected, act_acc = (stored, act_acc)
    attn_grad = act_acc.astype(jnp.bfloat16)
    columns = lax.all_to_all(collected, "dp", split_axis=1, concat_axis=0, tiled=True)
    column_width = columns.shape[1]
    portion = lax.all_gather(attn_out, "dp", axis=0, tiled=True)
    blocks_in = portion.shape[0] // tokens_dev
    head_block = portion.reshape(blocks_in, tokens_dev, head_cols)
    column_part = columns.reshape(blocks_in, tokens_dev, column_width)
    shares = (
        jnp.einsum("bti,btj->bij", head_block, column_part, preferred_element_type=jnp.float32)
        * replica_scale
    )
    rounded = lax.optimization_barrier(shares.astype(jnp.bfloat16))
    grad_block = jnp.sum(rounded.astype(jnp.float32), axis=0)
    weight_grad = lax.psum(grad_block.astype(jnp.bfloat16), "cuts").astype(jnp.float32)
    return (block_out, attn_grad, weight_grad)


def solution(mesh):
    placed = (
        P(("cuts", "dp"), "mp"),
        P("mp", None),
        P(("cuts", "dp", "mp"), None),
        P(("cuts", "dp", "mp"), None),
        P(),
    )
    return jax.shard_map(
        per_device,
        mesh=mesh,
        in_specs=placed,
        out_specs=(P(("cuts", "dp", "mp"), None), P(("cuts", "dp"), "mp"), P("mp", "dp")),
        check_vma=False,
    )
```

profile of v0, /device:TPU:1, one launch (start us, length us, event | category | flops | bytes accessed | tf_op | source)
XLA Modules:
  0.0 297.5 jit_solution(12666012923011112041)
XLA Ops:
  7.2 0.0 reduce-scatter.2.cloned.1.call-start
  7.2 10.3 %convolution_convert_fusion = bf16[128,6144]{1,0:T(8,128)(2,1)} fusion(bf16[128,1536]{1,0:T(8,128)(2,1)} %param.5, bf16[1536,6144]{1,0:T(8,128)(2,1)} %param.6), kind=kOutput, calls=%fused_computation.3 | convolution fusion | flops 2416705536 | bytes 20840448 | tf_op jit(solution)/shard_map/dot_general | solution.py:28
  17.5 0.0 copy-start
  17.5 0.0 copy-start.4
  17.5 0.0 reduce-scatter.2.cloned.1.call-update
  17.5 0.0 copy-start.3
  17.5 0.0 all-gather.3.cloned.1.call-start
  17.6 11.7 %reduce-scatter.2.cloned.1.call-done = bf16[64,6144]{1,0:T(8,128)(2,1)} async-done(((bf16[128,6144]{1,0:T(8,128)(2,1)}), bf16[64,6144]{1,0:T(8,128)(2,1)}) %reduce-scatter.2.cloned.1.call-update) | async-done | bytes 786448 | tf_op jit(solution)/shard_map/reduce_scatter | solution.py:27
  29.3 0.0 copy-done
  29.3 1.5 fusion.4
  30.8 0.0 copy-done.1
  30.8 0.4 multiply_reduce_fusion.1
  31.3 0.0 copy-done.4
  31.3 0.0 copy-done.3
  31.3 0.8 fusion.3
  32.1 1.9 multiply_convert_fusion
  34.0 0.0 all-gather.3.cloned.1.call-update
  34.1 0.0 all-gather.5.cloned.1.call-start
  34.1 0.7 all-gather.5.cloned.1.call-update
  34.8 10.4 %all-gather.3.cloned.1.call-done = bf16[128,6144]{1,0:T(8,128)(2,1)} async-done(((bf16[64,6144]{1,0:T(8,128)(2,1)}), bf16[128,6144]{1,0:T(8,128)(2,1)}) %all-gather.3.cloned.1.call-update) | async-done | bytes 1572880 | tf_op jit(solution)/shard_map/all_gather | solution.py:36
  45.2 2.6 copy.11
  47.8 3.7 %all-to-all-start = ((bf16[128,4,1536]{0,2,1:T(8,128)(2,1)}), bf16[128,4,1536]{0,2,1:T(8,128)(2,1)S(1)}, u32[]{:S(2)}, u32[]{:S(2)}) async-start(bf16[128,4,1536]{0,2,1:T(8,128)(2,1)} %bitcast), calls=%async_computation.1 | async-start | bytes 3145728 | tf_op jit(solution)/shard_map/all_to_all | solution.py:43
  51.5 0.1 all-reduce.2.cloned.1.call-start
  51.6 35.8 %all-gather.5.cloned.1.call-done = bf16[512,1536]{1,0:T(8,128)(2,1)} async-done(((bf16[128,1536]{1,0:T(8,128)(2,1)}), bf16[512,1536]{1,0:T(8,128)(2,1)}) %all-gather.5.cloned.1.call-update) | async-done | bytes 1572880 | tf_op jit(solution)/shard_map/all_gather | solution.py:45
  87.3 0.0 all-to-all-done
  87.3 10.6 %fusion.1 = bf16[4,1536,1536]{1,2,0:T(8,128)(2,1)} fusion(bf16[4,128,1536]{2,1,0:T(8,128)(2,1)} %bitcast.12, bf16[128,4,1536]{0,2,1:T(8,128)(2,1)S(1)} %all-to-all-done), kind=kOutput, calls=%fused_computation.2 | convolution fusion | flops 2434793472 | bytes 22020096 | tf_op jit(solution)/shard_map/bti,btj->bij/dot_general | solution.py:50
  97.9 13.5 %reduce_sum.52 = bf16[1536,1536]{0,1:T(8,128)(2,1)} reduce(bf16[4,1536,1536]{1,2,0:T(8,128)(2,1)} %fusion.1, bf16[]{:T(256)} %constant.13.clone.1), dimensions={0}, to_apply=%region_5.0 | reduce | flops 7077888 | bytes 23592962 | tf_op jit(solution)/shard_map/reduce_sum | solution.py:54
  111.5 0.0 all-reduce.2.cloned.1.call-update
  111.5 1.4 copy-done.2
  112.9 14.3 %convolution_convert_fusion.1 = bf16[128,1536]{1,0:T(8,128)(2,1)} fusion(bf16[128,6144]{1,0:T(8,128)(2,1)S(1)} %copy-done.2, bf16[1536,6144]{1,0:T(8,128)(2,1)} %param.6), kind=kOutput, calls=%fused_computation.4 | convolution fusion | flops 2416115712 | bytes 20840448 | tf_op jit(solution)/shard_map/dot_general | solution.py:38
  127.2 156.4 %all-reduce.2.cloned.1.call-done = bf16[1536,1536]{0,1:T(8,128)(2,1)} async-done(((bf16[1536,1536]{0,1:T(8,128)(2,1)}), bf16[1536,1536]{0,1:T(8,128)(2,1)}) %all-reduce.2.cloned.1.call-update) | async-done | bytes 4718608 | tf_op jit(solution)/shard_map/psum | solution.py:55
  283.6 7.4 %copy.10 = f32[1536,1536]{1,0:T(8,128)} copy(bf16[1536,1536]{0,1:T(8,128)(2,1)} %all-reduce.2.cloned.1.call-done) | data formatting | bytes 14155776
  (5 shorter events, 0.0 us)
Async XLA Ops:
  7.2 22.1 %reduce-scatter.2.cloned.1.call-start = ((), (), s32[]{:S(2)}) async-start(), calls=%async_computation.2 | async-start | bytes 2359296 | tf_op jit(solution)/shard_map/reduce_scatter | solution.py:27
  17.5 11.8 %copy-start = (bf16[64,6144]{1,0:T(8,128)(2,1)S(1)}, bf16[64,6144]{1,0:T(8,128)(2,1)}, u32[]{:S(2)}) copy-start(bf16[64,6144]{1,0:T(8,128)(2,1)} %param.7) | copy-start | bytes 2359300
  17.5 13.8 %copy-start.4 = (f32[6144]{0:T(1024)S(1)}, f32[6144]{0:T(1024)}, u32[]{:S(2)}) copy-start(f32[6144]{0:T(1024)} %param.9) | copy-start | bytes 73732
  17.5 13.8 %copy-start.3 = (bf16[64,6144]{1,0:T(8,128)(2,1)S(1)}, bf16[64,6144]{1,0:T(8,128)(2,1)}, u32[]{:S(2)}) copy-start(bf16[64,6144]{1,0:T(8,128)(2,1)} %param.8) | copy-start | bytes 2359300
  17.5 27.7 %all-gather.3.cloned.1.call-start = ((), (), s32[]{:S(2)}) async-start(), calls=%async_computation.3 | async-start | bytes 2359296 | tf_op jit(solution)/shard_map/all_gather | solution.py:36
  29.3 1.5 copy-start.1
  34.1 53.3 %all-gather.5.cloned.1.call-start = ((), (), s32[]{:S(2)}) async-start(), calls=%async_computation.4 | async-start | bytes 1966080 | tf_op jit(solution)/shard_map/all_gather | solution.py:45
  47.8 39.6 %all-to-all-start = ((bf16[128,4,1536]{0,2,1:T(8,128)(2,1)}), bf16[128,4,1536]{0,2,1:T(8,128)(2,1)S(1)}, u32[]{:S(2)}, u32[]{:S(2)}) async-start(bf16[128,4,1536]{0,2,1:T(8,128)(2,1)} %bitcast), calls=%async_computation.1 | async-start | bytes 3145728 | tf_op jit(solution)/shard_map/all_to_all | solution.py:43
  51.5 232.1 %all-reduce.2.cloned.1.call-start = ((), (), s32[]{:S(2)}) async-start(), calls=%async_computation.5 | async-start | bytes 9437184 | tf_op jit(solution)/shard_map/psum | solution.py:55
  111.5 1.4 copy-start.2
Sparse Core Ops, SparseCore 0:
  17.6 11.6 reduce-scatter.1
  34.2 10.9 all-gather.2
  47.0 40.2 all-gather.4
  111.6 171.9 all-reduce.1
where the time goes:
time: 299 us; the launch traced here: 298 us
  waiting for transfers between devices  215 us (72%)
  matrix products  35.2 us (12%)
  other arithmetic  18.3 us (6%)
  between operations  13.8 us (5%)
  local copies, waits for them, and re-layouts  11.4 us (4%)
  starting transfers between devices  3.91 us (1%)
    psum x1, waiting for transfers between devices, per_device(): lax.psum(grad_block.astype(jnp.bfloat16), 'cuts').astype(jnp.float32)  156 us
    all_gather x1, waiting for transfers between devices, per_device(): portion = lax.all_gather(attn_out, 'dp', axis=0, tiled=True)  35.8 us
    dot_general x1, matrix products, per_device(): lax.dot_general(portion, out_weight, (((1,), (1,)), ((), ())), preferred_...  14.3 us
    reduce_sum x1, other arithmetic, per_device(): grad_block = jnp.sum(rounded.astype(jnp.float32), axis=0)  13.5 us
    reduce_scatter x1, waiting for transfers between devices, per_device(): lax.psum_scatter(jnp.dot(attn_out, out_weight, preferred_element_type=jnp...  11.7 us
    dot_general x1, matrix products, per_device(): jnp.einsum('bti,btj->bij', head_block, column_part, preferred_element_typ...  10.6 us
    all_gather x1, waiting for transfers between devices, per_device(): portion = lax.all_gather(cotangent, 'mp', axis=0, tiled=True)  10.4 us
    dot_general x1, matrix products, per_device(): jnp.dot(attn_out, out_weight, preferred_element_type=jnp.float32)  10.3 us
  transfers between devices with their start and end apart: 5, of which 4 were waited for; matrix products, arithmetic and copies ran while one was open for 6% of the time, Pallas kernels for 0%

commit v1 on v0

--- a/solution.py
+++ b/solution.py
@@ -1,6 +1,10 @@
+import functools
+
 import jax
 import jax.numpy as jnp
 from jax import lax
+from jax.experimental import pallas as pl
+from jax.experimental.pallas import tpu as pltpu
 from jax.sharding import PartitionSpec as P
 
 epsilon = 1e-06
@@ -56,7 +60,347 @@
     return (block_out, attn_grad, weight_grad)
 
 
+MESH = pl.DeviceIdType.MESH
+
+
+def remote(src, dst, send_sem, recv_sem, **where):
+    return pltpu.make_async_remote_copy(
+        src_ref=src, dst_ref=dst, send_sem=send_sem, recv_sem=recv_sem, device_id=where, device_id_type=MESH
+    )
+
+
+def fused(
+    nz, ndp, chunk, attn_h, w_h, res_h, tgt_h, gain_h, blk_o, agrad_o, wgrad_o,
+    w_v, a_v, rows_v, cot_v, part, part_in, res_v, tgt_v, gain_v, blk_v, agrad_v, acc,
+    ld_s, w_s, p_s, p_r, au_s, ad_s, az_r, ap_s, ap_r, cp_s, cq_s, cq_r, cu_s, cd_s, c_r, ce_s, ce_r, o_s,
+):
+    z, dp, m = lax.axis_index("cuts"), lax.axis_index("dp"), lax.axis_index("mp")
+    other = 1 - m
+    tok, heads = attn_h.shape
+    half, width = res_h.shape
+    cols = width // ndp
+    chunks = width // chunk
+    has_up, has_down = z + 1 < nz, z >= 1
+    scale = 1.0 / (nz * ndp)
+
+    loads = [
+        pltpu.make_async_copy(attn_h, a_v.at[z, dp], ld_s.at[0]),
+        pltpu.make_async_copy(res_h, res_v, ld_s.at[1]),
+        pltpu.make_async_copy(tgt_h, tgt_v, ld_s.at[2]),
+        pltpu.make_async_copy(gain_h, gain_v, ld_s.at[3]),
+    ]
+    loads[0].start()
+
+    def w_load(c):
+        at = pl.ds(pl.multiple_of(c * chunk, chunk), chunk)
+        return pltpu.make_async_copy(w_h.at[:, at], w_v.at[:, at], w_s.at[c])
+
+    for c in range(chunks):
+        w_load(c).start()
+    for load in loads[1:]:
+        load.start()
+
+    barrier = pltpu.get_barrier_semaphore()
+    pl.semaphore_signal(barrier, inc=1, device_id={"mp": other}, device_id_type=MESH)
+    for k in range(1, ndp):
+        pl.semaphore_signal(barrier, inc=1, device_id={"dp": lax.rem(dp + k, ndp)}, device_id_type=MESH)
+
+    @pl.when(has_up)
+    def _():
+        pl.semaphore_signal(barrier, inc=1, device_id={"cuts": z + 1}, device_id_type=MESH)
+
+    @pl.when(has_down)
+    def _():
+        pl.semaphore_signal(barrier, inc=1, device_id={"cuts": z - 1}, device_id_type=MESH)
+
+    pl.semaphore_wait(barrier, ndp + jnp.where(has_up, 1, 0) + jnp.where(has_down, 1, 0))
+
+    def a_up(l):
+        return remote(a_v.at[l, dp], a_v.at[l, dp], au_s.at[l], az_r.at[l], cuts=z + 1)
+
+    def a_down(l):
+        return remote(a_v.at[l, dp], a_v.at[l, dp], ad_s.at[l], az_r.at[l], cuts=z - 1)
+
+    def a_plane(l, k):
+        return remote(a_v.at[l, dp], a_v.at[l, dp], ap_s.at[l, k], ap_r.at[l, dp], dp=lax.rem(dp + k, ndp))
+
+    def a_plane_in(l, k):
+        src = lax.rem(dp + ndp - k, ndp)
+        return remote(a_v.at[l, src], a_v.at[l, src], ap_s.at[l, k], ap_r.at[l, src], dp=src)
+
+    def c_up(l, d, src=None):
+        return remote(cot_v.at[l, d, m] if src is None else src, cot_v.at[l, d, m], cu_s.at[l, d], c_r.at[l, d], cuts=z + 1)
+
+    def c_down(l, d, src=None):
+        return remote(cot_v.at[l, d, m] if src is None else src, cot_v.at[l, d, m], cd_s.at[l, d], c_r.at[l, d], cuts=z - 1)
+
+    def c_pair(l, d):
+        return remote(cot_v.at[l, d, m], cot_v.at[l, d, m], ce_s.at[l, d], ce_r.at[l, d], mp=other)
+
+    def c_pair_in(l, d):
+        return remote(cot_v.at[l, d, other], cot_v.at[l, d, other], ce_s.at[l, d], ce_r.at[l, d], mp=other)
+
+    def a_hop(k):
+        low, high = z - k, z + k
+
+        @pl.when(low >= 0)
+        def _():
+            a_up(low).wait_recv()
+
+            @pl.when(has_up)
+            def _():
+                a_up(low).start()
+
+        @pl.when(high < nz)
+        def _():
+            a_down(high).wait_recv()
+
+            @pl.when(has_down)
+            def _():
+                a_down(high).start()
+
+    def both(k, f):
+        pl.when(z - k >= 0)(lambda: f(z - k))
+        pl.when(z + k < nz)(lambda: f(z + k))
+
+    loads[0].wait()
+
+    @pl.when(has_up)
+    def _():
+        a_up(z).start()
+
+    @pl.when(has_down)
+    def _():
+        a_down(z).start()
+
+    for k in range(1, ndp):
+        a_plane(z, k).start()
+
+    def p_send(c):
+        at = pl.ds(pl.multiple_of(c * chunk, chunk), chunk)
+        return remote(part.at[other, :, at], part_in.at[:, at], p_s.at[c], p_r.at[c], mp=other)
+
+    @pl.loop(0, chunks)
+    def _(c):
+        at = pl.ds(pl.multiple_of(c * chunk, chunk), chunk)
+        w_load(c).wait()
+        value = jnp.dot(a_v[z, dp], w_v[:, at], preferred_element_type=jnp.float32).astype(jnp.bfloat16)
+        part[0, :, at] = value[:half]
+        part[1, :, at] = value[half:]
+        p_send(c).start()
+
+    a_hop(1)
+    for load in loads[1:]:
+        load.wait()
+
+    @pl.loop(0, chunks)
+    def _(c):
+        p_send(c).wait()
+
+    step = 16
+    gain = gain_v[...]
+
+    @pl.loop(0, half // step)
+    def _(i):
+        at = pl.ds(pl.multiple_of(i * step, step), step)
+        stream = (
+            part[m, at, :].astype(jnp.float32) + part_in[at, :].astype(jnp.float32) + res_v[at, :].astype(jnp.float32)
+        )
+        blk_v[at, :] = stream.astype(jnp.bfloat16)
+        center = stream - jnp.mean(stream, axis=1, keepdims=True)
+        inv_std = lax.rsqrt(jnp.mean(center * center, axis=1, keepdims=True) + epsilon)
+        normed = center * inv_std
+        gain_err = (normed * gain - tgt_v[at, :].astype(jnp.float32)) * gain
+        bracket = (
+            gain_err
+            - jnp.mean(gain_err, axis=1, keepdims=True)
+            - normed * jnp.mean(gain_err * normed, axis=1, keepdims=True)
+        )
+        cot = (inv_std * bracket).astype(jnp.bfloat16)
+        for d in range(ndp):
+            rows_v[d, m, at, :] = cot[:, d * cols : (d + 1) * cols]
+
+    def c_plane(k):
+        to = lax.rem(dp + k, ndp)
+        return remote(rows_v.at[to, m], cot_v.at[z, dp, m], cp_s.at[k], c_r.at[z, dp], dp=to)
+
+    def c_rows():
+        return remote(rows_v.at[:, m], rows_v.at[:, m], cq_s.at[0], cq_r.at[0], mp=other)
+
+    def c_rows_in():
+        return remote(rows_v.at[:, other], rows_v.at[:, other], cq_s.at[0], cq_r.at[0], mp=other)
+
+    for k in range(1, ndp):
+        c_plane(k).start()
+    own = rows_v.at[dp, m]
+
+    @pl.when(has_up)
+    def _():
+        c_up(z, dp, own).start()
+
+    @pl.when(has_down)
+    def _():
+        c_down(z, dp, own).start()
+
+    c_rows().start()
+    blk_copy = pltpu.make_async_copy(blk_v, blk_o, ld_s.at[1])
+    blk_copy.start()
+    cot_v[z, dp, m] = rows_v[dp, m]
+
+    both(1, lambda l: [a_plane(l, k).start() for k in range(1, ndp)] and None)
+    c_rows_in().wait_recv()
+    cot_v[z, dp, other] = rows_v[dp, other]
+
+    def c_forward(l, d, up, down):
+        pl.when(up)(lambda: c_up(l, d).start())
+        pl.when(down)(lambda: c_down(l, d).start())
+        c_pair(l, d).start()
+
+    for k in range(1, ndp):
+        d = lax.rem(dp + ndp - k, ndp)
+        c_up(z, d).wait_recv()
+        c_forward(z, d, has_up, has_down)
+    for k in range(2, nz):
+        a_hop(k)
+        both(k, lambda l: [a_plane(l, j).start() for j in range(1, ndp)] and None)
+
+    tile = 512 if heads % 512 == 0 else heads
+
+    @pl.loop(0, heads // tile)
+    def _(j):
+        at = pl.ds(pl.multiple_of(j * tile, tile), tile)
+        total = jnp.zeros((tok, tile), jnp.float32)
+        for d in range(ndp):
+            total += lax.dot_general(
+                rows_v[d].reshape(tok, cols), w_v[at, d * cols : (d + 1) * cols], (((1,), (1,)), ((), ())),
+                preferred_element_type=jnp.float32,
+            )
+        agrad_v[:, at] = total.astype(jnp.bfloat16)
+
+    agrad_copy = pltpu.make_async_copy(agrad_v, agrad_o, ld_s.at[2])
+    agrad_copy.start()
+
+    wide = 256 if heads % 256 == 0 else heads
+
+    def group(l, first):
+        for k in range(1, ndp):
+            a_plane_in(l, k).wait_recv()
+
+        @pl.loop(0, heads // wide)
+        def _(j):
+            at = pl.ds(pl.multiple_of(j * wide, wide), wide)
+            value = scale * lax.dot_general(
+                a_v[l, :, :, at].reshape(ndp * tok, wide), cot_v[l].reshape(ndp * tok, cols), (((0,), (0,)), ((), ())),
+                preferred_element_type=jnp.float32,
+            )
+            acc[at, :] = value if first else acc[at, :] + value
+
+    for k in range(1, ndp):
+        c_pair_in(z, lax.rem(dp + ndp - k, ndp)).wait_recv()
+    group(z, True)
+
+    @pl.loop(1, nz)
+    def _(k):
+        for j in range(ndp):
+            d = lax.rem(dp + ndp - j, ndp)
+
+            @pl.when(z - k >= 0)
+            def _():
+                c_up(z - k, d).wait_recv()
+                c_forward(z - k, d, has_up, False)
+
+            @pl.when(z + k < nz)
+            def _():
+                c_down(z + k, d).wait_recv()
+                c_forward(z + k, d, False, has_down)
+
+        def finish(l):
+            for j in range(ndp):
+                c_pair_in(l, j).wait_recv()
+            group(l, False)
+
+        both(k, finish)
+
+    out = pltpu.make_async_copy(acc, wgrad_o, o_s.at[0])
+    out.start()
+
+    @pl.loop(0, nz)
+    def _(l):
+        @pl.when(has_up & (l <= z))
+        def _():
+            a_up(l).wait_send()
+            for d in range(ndp):
+                c_up(l, d).wait_send()
+
+        @pl.when(has_down & (l >= z))
+        def _():
+            a_down(l).wait_send()
+            for d in range(ndp):
+                c_down(l, d).wait_send()
+
+        for k in range(1, ndp):
+            a_plane(l, k).wait_send()
+            c_pair(l, lax.rem(dp + k, ndp)).wait_send()
+
+        @pl.when(l != z)
+        def _():
+            c_pair(l, dp).wait_send()
+
+    for k in range(1, ndp):
+        c_plane(k).wait_send()
+    c_rows().wait_send()
+    blk_copy.wait()
+    agrad_copy.wait()
+    out.wait()
+
+
+def fused_device(nz, ndp, attn_out, out_weight, residual, target, norm_gain):
+    tok, heads = attn_out.shape
+    half, width = residual.shape
+    cols = width // ndp
+    chunk = 512 if width % 512 == 0 else 128
+    chunks = width // chunk
+    bf16, f32 = jnp.bfloat16, jnp.float32
+    dma = pltpu.SemaphoreType.DMA
+    any_space = pl.BlockSpec(memory_space=pl.ANY)
+    return pl.pallas_call(
+        functools.partial(fused, nz, ndp, chunk),
+        out_shape=(
+            jax.ShapeDtypeStruct((half, width), bf16),
+            jax.ShapeDtypeStruct((tok, heads), bf16),
+            jax.ShapeDtypeStruct((heads, cols), f32),
+        ),
+        in_specs=[any_space] * 5,
+        out_specs=(any_space,) * 3,
+        scratch_shapes=[
+            pltpu.VMEM((heads, width), bf16),
+            pltpu.VMEM((nz, ndp, tok, heads), bf16),
+            pltpu.VMEM((ndp, 2, half, cols), bf16),
+            pltpu.VMEM((nz, ndp, 2, half, cols), bf16),
+            pltpu.VMEM((2, half, width), bf16),
+            pltpu.VMEM((half, width), bf16),
+            pltpu.VMEM((half, width), bf16),
+            pltpu.VMEM((half, width), bf16),
+            pltpu.VMEM((1, width), f32),
+            pltpu.VMEM((half, width), bf16),
+            pltpu.VMEM((tok, heads), bf16),
+            pltpu.VMEM((heads, cols), f32),
+            dma((4,)), dma((chunks,)), dma((chunks,)), dma((chunks,)),
+            dma((nz,)), dma((nz,)), dma((nz,)), dma((nz, ndp)), dma((nz, ndp)),
+            dma((ndp,)), dma((1,)), dma((1,)),
+            dma((nz, ndp)), dma((nz, ndp)), dma((nz, ndp)), dma((nz, ndp)), dma((nz, ndp)), dma((1,)),
+        ],
+        compiler_params=pltpu.CompilerParams(
+            collective_id=0, has_side_effects=True, vmem_limit_bytes=66 * 1000 * 1000
+        ),
+    )(attn_out, out_weight, residual, target, norm_gain.reshape(1, width))
+
+
 def solution(mesh):
+    if mesh.shape["mp"] == 2:
+        body = functools.partial(fused_device, mesh.shape["cuts"], mesh.shape["dp"])
+    else:
+        body = per_device
     placed = (
         P(("cuts", "dp"), "mp"),
         P("mp", None),
@@ -65,7 +409,7 @@
         P(),
     )
     return jax.shard_map(
-        per_device,
+        body,
         mesh=mesh,
         in_specs=placed,
         out_specs=(P(("cuts", "dp", "mp"), None), P(("cuts", "dp"), "mp"), P("mp", "dp")),

time: 299 us -> 112 us (0.37)
  waiting for transfers between devices: 215 us -> 0 us
  Pallas kernels: 0 us -> 99.5 us
  matrix products: 35.2 us -> 0 us
  other arithmetic: 18.3 us -> 0 us
  between operations: 13.8 us -> 0.64 us
  starting transfers between devices: 3.91 us -> 0 us
    psum x1 -> x0, waiting for transfers between devices: 156 us -> none  [per_device(): lax.psum(grad_block.astype(jnp.bfloat16), 'cuts').astype(jnp.float32)]
    pallas_call x0 -> x1, Pallas kernels: none -> 99.5 us  [fused_device(): pl.pallas_call(functools.partial(fused, nz, ndp, chunk), out_shape=(jax.S...]
    all_gather x2 -> x0, waiting for transfers between devices: 46.2 us -> none  [the longest x1 35.8 us: per_device(): portion = lax.all_gather(attn_out, 'dp', axis=0, tiled=True)]
    dot_general x3 -> x0, matrix products: 35.2 us -> none  [the longest x1 14.3 us: per_device(): lax.dot_general(portion, out_weight, (((1,), (1,)), ((), ())), preferred_...]
    reduce_sum x4 -> x0, other arithmetic: 16.3 us -> none  [the longest x1 13.5 us: per_device(): grad_block = jnp.sum(rounded.astype(jnp.float32), axis=0)]
    reduce_scatter x1 -> x0, waiting for transfers between devices: 11.7 us -> none  [per_device(): lax.psum_scatter(jnp.dot(attn_out, out_weight, preferred_element_type=jnp...]
    all_to_all x1 -> x0, starting transfers between devices: 3.71 us -> none  [per_device(): lax.all_to_all(collected, 'dp', split_axis=1, concat_axis=0, tiled=True)]
    unnamed x11 -> x3, local copies, waits for them, and re-layouts: 8.8 us -> 12.1 us
  transfers between devices with their start and end apart: 5 -> 0, of which waited for: 4 -> 0; matrix products, arithmetic and copies ran while one was open for 6% -> 0% of each run, Pallas kernels for 0% -> 0%
where the time goes in v1:
time: 112 us
  Pallas kernels  99.5 us (89%)
  local copies, waits for them, and re-layouts  12.1 us (11%)
    pallas_call x1, Pallas kernels, fused_device(): pl.pallas_call(functools.partial(fused, nz, ndp, chunk), out_shape=(jax.S...  99.5 us
    unnamed x3, local copies, waits for them, and re-layouts  12.1 us

profile of v1, /device:TPU:1, one launch (start us, length us, event | category | flops | bytes accessed | tf_op | source)
XLA Modules:
  0.0 112.2 jit_solution(18050951345221081275)
XLA Ops:
  0.6 99.5 %shard_map.76 = (bf16[64,6144]{1,0:T(8,128)(2,1)}, bf16[128,1536]{1,0:T(8,128)(2,1)}, f32[1536,1536]{1,0:T(8,128)}) custom-call(bf16[128,1536]{1,0:T(8,128)(2,1)} %attn_h.1, bf16[1536,6144]{1,0:T(8,128)(2,1)} %w_h.1, bf16[64,6144]{1,0:T(8,128)(2,1)} %res_h.1, bf16[64,6144]{1,0:T(8,128)(2,1)} %tgt_h.1, f32[1,6144]{1,0:T(1,128)} %bitcast.1), custom_call_target="tpu_custom_call" | custom-call | tf_op jit(solution)/shard_map/pallas_call | solution.py:366
  100.1 2.1 %copy.11 = bf16[64,6144]{1,0:T(8,128)(2,1)} copy(bf16[64,6144]{1,0:T(8,128)(2,1)} %get-tuple-element.6) | data formatting | bytes 1572864
  102.2 1.8 %copy.12 = bf16[128,1536]{1,0:T(8,128)(2,1)} copy(bf16[128,1536]{1,0:T(8,128)(2,1)} %get-tuple-element.7) | data formatting | bytes 786432
  104.0 8.3 %copy.13 = f32[1536,1536]{1,0:T(8,128)} copy(f32[1536,1536]{1,0:T(8,128)} %get-tuple-element.8) | data formatting | bytes 18874368

commit v2 on v1

--- a/solution.py
+++ b/solution.py
@@ -71,7 +71,7 @@
 
 def fused(
     nz, ndp, chunk, attn_h, w_h, res_h, tgt_h, gain_h, blk_o, agrad_o, wgrad_o,
-    w_v, a_v, rows_v, cot_v, part, part_in, res_v, tgt_v, gain_v, blk_v, agrad_v, acc,
+    w_v, a_v, rows_v, cot_v, part, part_in, res_v, tgt_v, gain_v, blk_v, agrad_v, acc, out_v,
     ld_s, w_s, p_s, p_r, au_s, ad_s, az_r, ap_s, ap_r, cp_s, cq_s, cq_r, cu_s, cd_s, c_r, ce_s, ce_r, o_s,
 ):
     z, dp, m = lax.axis_index("cuts"), lax.axis_index("dp"), lax.axis_index("mp")
@@ -282,7 +282,13 @@
 
     wide = 256 if heads % 256 == 0 else heads
 
-    def group(l, first):
+    far = jnp.maximum(z, nz - 1 - z)
+
+    def out_copy(j):
+        at = pl.ds(pl.multiple_of(j * wide, wide), wide)
+        return pltpu.make_async_copy(out_v.at[at, :], wgrad_o.at[at, :], o_s.at[j])
+
+    def group(l, first, last):
         for k in range(1, ndp):
             a_plane_in(l, k).wait_recv()
 
@@ -293,11 +299,17 @@
                 a_v[l, :, :, at].reshape(ndp * tok, wide), cot_v[l].reshape(ndp * tok, cols), (((0,), (0,)), ((), ())),
                 preferred_element_type=jnp.float32,
             )
-            acc[at, :] = value if first else acc[at, :] + value
+            value = value if first else acc[at, :] + value
+            acc[at, :] = value
+
+            @pl.when(last)
+            def _():
+                out_v[at, :] = value.astype(jnp.bfloat16)
+                out_copy(j).start()
 
     for k in range(1, ndp):
         c_pair_in(z, lax.rem(dp + ndp - k, ndp)).wait_recv()
-    group(z, True)
+    group(z, True, far == 0)
 
     @pl.loop(1, nz)
     def _(k):
@@ -317,12 +329,9 @@
         def finish(l):
             for j in range(ndp):
                 c_pair_in(l, j).wait_recv()
-            group(l, False)
+            group(l, False, (l == z + far) | ((l == z - far) & (z + far >= nz)))
 
         both(k, finish)
-
-    out = pltpu.make_async_copy(acc, wgrad_o, o_s.at[0])
-    out.start()
 
     @pl.loop(0, nz)
     def _(l):
@@ -351,7 +360,16 @@
     c_rows().wait_send()
     blk_copy.wait()
     agrad_copy.wait()
-    out.wait()
+
+    @pl.loop(0, heads // wide)
+    def _(j):
+        out_copy(j).wait()
+
+
+def widen(blk_i, agrad_i, wgrad_i, blk_o, agrad_o, wgrad_o):
+    blk_o[...] = blk_i[...]
+    agrad_o[...] = agrad_i[...]
+    wgrad_o[...] = wgrad_i[...].astype(jnp.float32)
 
 
 def fused_device(nz, ndp, attn_out, out_weight, residual, target, norm_gain):
@@ -360,15 +378,16 @@
     cols = width // ndp
     chunk = 512 if width % 512 == 0 else 128
     chunks = width // chunk
+    tiles = heads // 256 if heads % 256 == 0 else 1
     bf16, f32 = jnp.bfloat16, jnp.float32
     dma = pltpu.SemaphoreType.DMA
     any_space = pl.BlockSpec(memory_space=pl.ANY)
-    return pl.pallas_call(
+    blk, agrad, wgrad = pl.pallas_call(
         functools.partial(fused, nz, ndp, chunk),
         out_shape=(
             jax.ShapeDtypeStruct((half, width), bf16),
             jax.ShapeDtypeStruct((tok, heads), bf16),
-            jax.ShapeDtypeStruct((heads, cols), f32),
+            jax.ShapeDtypeStruct((heads, cols), bf16),
         ),
         in_specs=[any_space] * 5,
         out_specs=(any_space,) * 3,
@@ -385,15 +404,34 @@
             pltpu.VMEM((half, width), bf16),
             pltpu.VMEM((tok, heads), bf16),
             pltpu.VMEM((heads, cols), f32),
+            pltpu.VMEM((heads, cols), bf16),
             dma((4,)), dma((chunks,)), dma((chunks,)), dma((chunks,)),
             dma((nz,)), dma((nz,)), dma((nz,)), dma((nz, ndp)), dma((nz, ndp)),
             dma((ndp,)), dma((1,)), dma((1,)),
-            dma((nz, ndp)), dma((nz, ndp)), dma((nz, ndp)), dma((nz, ndp)), dma((nz, ndp)), dma((1,)),
+            dma((nz, ndp)), dma((nz, ndp)), dma((nz, ndp)), dma((nz, ndp)), dma((nz, ndp)), dma((tiles,)),
         ],
         compiler_params=pltpu.CompilerParams(
             collective_id=0, has_side_effects=True, vmem_limit_bytes=66 * 1000 * 1000
         ),
     )(attn_out, out_weight, residual, target, norm_gain.reshape(1, width))
+    parts = tiles if width % (tiles * 128) == 0 and heads % (tiles * 128) == 0 else 1
+    specs = [
+        pl.BlockSpec((half, width // parts), lambda i: (0, i)),
+        pl.BlockSpec((tok, heads // parts), lambda i: (0, i)),
+        pl.BlockSpec((heads // parts, cols), lambda i: (i, 0)),
+    ]
+    return pl.pallas_call(
+        widen,
+        grid=(parts,),
+        out_shape=(
+            jax.ShapeDtypeStruct((half, width), bf16),
+            jax.ShapeDtypeStruct((tok, heads), bf16),
+            jax.ShapeDtypeStruct((heads, cols), f32),
+        ),
+        in_specs=specs,
+        out_specs=tuple(specs),
+        compiler_params=pltpu.CompilerParams(vmem_limit_bytes=32 * 1000 * 1000),
+    )(blk, agrad, wgrad)
 
 
 def solution(mesh):

time: 112 us -> 107 us (0.955)
  local copies, waits for them, and re-layouts: 12.1 us -> 4.46 us
  Pallas kernels: 99.5 us -> 102 us
    unnamed x3 -> x6, local copies, waits for them, and re-layouts: 12.1 us -> 4.46 us
    pallas_call x0 -> x1, Pallas kernels: none -> 4.49 us  [fused_device(): pl.pallas_call(widen, grid=(parts,), out_shape=(jax.ShapeDtypeStruct((hal...]
    pallas_call x1, Pallas kernels: 99.5 us -> 97.3 us  [fused_device(): pl.pallas_call(functools.partial(fused, nz, ndp, chunk), out_shape=(jax.S...]
where the time goes in v2:
time: 107 us
  Pallas kernels  102 us (95%)
  local copies, waits for them, and re-layouts  4.46 us (4%)
    pallas_call x1, Pallas kernels, fused_device(): pl.pallas_call(functools.partial(fused, nz, ndp, chunk), out_shape=(jax.S...  97.3 us
    pallas_call x1, Pallas kernels, fused_device(): pl.pallas_call(widen, grid=(parts,), out_shape=(jax.ShapeDtypeStruct((hal...  4.49 us
    unnamed x6, local copies, waits for them, and re-layouts  4.46 us

profile of v2, /device:TPU:1, one launch (start us, length us, event | category | flops | bytes accessed | tf_op | source)
XLA Modules:
  0.0 106.9 jit_solution(7332308724305441669)
XLA Ops:
  0.6 97.3 %shard_map.76 = (bf16[64,6144]{1,0:T(8,128)(2,1)}, bf16[128,1536]{1,0:T(8,128)(2,1)}, bf16[1536,1536]{1,0:T(8,128)(2,1)}) custom-call(bf16[128,1536]{1,0:T(8,128)(2,1)} %attn_h.1, bf16[1536,6144]{1,0:T(8,128)(2,1)} %w_h.1, bf16[64,6144]{1,0:T(8,128)(2,1)} %res_h.1, bf16[64,6144]{1,0:T(8,128)(2,1)} %tgt_h.1, f32[1,6144]{1,0:T(1,128)} %bitcast.1), custom_call_target="tpu_custom_call" | custom-call | tf_op jit(solution)/shard_map/pallas_call | solution.py:385
  97.9 0.0 copy-start
  98.0 2.3 %copy-done = bf16[1536,1536]{1,0:T(8,128)(2,1)S(1)} copy-done((bf16[1536,1536]{1,0:T(8,128)(2,1)S(1)}, bf16[1536,1536]{1,0:T(8,128)(2,1)}, u32[]{:S(2)}) %copy-start) | copy-done | bytes 4718616
  100.3 0.0 copy-start.1
  100.3 1.1 %copy-done.1 = bf16[64,6144]{1,0:T(8,128)(2,1)S(1)} copy-done((bf16[64,6144]{1,0:T(8,128)(2,1)S(1)}, bf16[64,6144]{1,0:T(8,128)(2,1)}, u32[]{:S(2)}) %copy-start.1) | copy-done | bytes 786456
  101.4 0.0 copy-start.2
  101.4 1.0 copy-done.2
  102.4 4.5 %shard_map.77 = (bf16[64,6144]{1,0:T(8,128)(2,1)}, bf16[128,1536]{1,0:T(8,128)(2,1)}, f32[1536,1536]{1,0:T(8,128)}) custom-call(bf16[64,6144]{1,0:T(8,128)(2,1)S(1)} %copy-done.1, bf16[128,1536]{1,0:T(8,128)(2,1)S(1)} %copy-done.2, bf16[1536,1536]{1,0:T(8,128)(2,1)S(1)} %copy-done), custom_call_target="tpu_custom_call" | custom-call | tf_op jit(solution)/shard_map/pallas_call | solution.py:423
Async XLA Ops:
  97.9 2.3 %copy-start = (bf16[1536,1536]{1,0:T(8,128)(2,1)S(1)}, bf16[1536,1536]{1,0:T(8,128)(2,1)}, u32[]{:S(2)}) copy-start(bf16[1536,1536]{1,0:T(8,128)(2,1)} %get-tuple-element.8.wgrad_i) | copy-start | bytes 14155780
  100.3 1.1 %copy-start.1 = (bf16[64,6144]{1,0:T(8,128)(2,1)S(1)}, bf16[64,6144]{1,0:T(8,128)(2,1)}, u32[]{:S(2)}) copy-start(bf16[64,6144]{1,0:T(8,128)(2,1)} %get-tuple-element.6.blk_i) | copy-start | bytes 2359300
  101.4 1.0 copy-start.2
